TPU v7x, 128 devices: a whole 4x4x4 slice. The times are simulated.
128 devices in a mesh: mx: 4 (over z), my: 4 (over y_hi, core), col: 8 (over y_lo, x).
Axes of the slice: x: 4, y: 4 (y_hi: 2, y_lo: 2; y = y_hi * 2 + y_lo), z: 4, core: 2. Of those that a mesh axis runs over, the one named last changes fastest.
Arguments:
- spectrum: float32 [2, 16, 128, 32, 512], P(None, 'col', None, 'mx', 'my'), may hold values from -6 to 6
- core_tensor: float32 [2, 64, 64, 16, 16, 16], P(None, 'col', None, ('mx', 'my')), may hold values from -0.01171875 to 0.01171875
- input_factor: float32 [128, 64], replicated, may hold values from -0.5 to 0.5
- output_factor: float32 [128, 64], replicated, may hold values from -0.75 to 0.75
- first_factor: float32 [32, 16], P('mx'), may hold values from -5 to 5
- second_factor: float32 [32, 16], P('my'), may hold values from -5 to 5
- third_factor: float32 [16, 16], replicated, may hold values from -5 to 5
Outputs:
- mixed_modes: float32 [2, 16, 128, 32, 512], P(None, 'col', None, 'mx', 'my')
All inputs are finite; a program needn't handle non-finite values.
Results may differ from a plain program's by a relative error of at most 0.00007.
Values sent between devices are 32-bit elements; how exact they have to be, the bound alone decides.
No kernel may reach another device: no remote copies, remote signals or barrier semaphores. Data moves between devices by JAX's collectives and lax.ppermute only.
A program may use at most 128 MiB of HBM per device.

v0:
```python
import jax
import jax.numpy as jnp
from jax import lax
from jax.sharding import PartitionSpec as P

precise = lax.Precision.HIGHEST


def per_device(
    spectrum, core_tensor, input_factor, output_factor, first_factor, second_factor, third_factor
):
    rank_local = core_tensor.shape[1]
    rank_out = core_tensor.shape[2]
    rows_first = first_factor.shape[0]
    rank_second = second_factor.shape[1]
    modes_third = third_factor.shape[0]
    core_third = jnp.einsum("cpqstu,zu->cpqstz", core_tensor, third_factor, precision=precise)
    core_third = core_third.reshape(
        2, rank_local, rank_out, core_tensor.shape[3], rank_second * modes_third
    )
    core_gathered = lax.all_gather(core_third, ("mx", "my"), axis=3, tiled=True)
    weight_first = jnp.einsum("cpqsm,ks->cpqkm", core_gathered, first_factor, precision=precise)
    weight_first = weight_first.reshape(
        2, rank_local, rank_out, rows_first, rank_second, modes_third
    )
    mode_weight = jnp.einsum("cpqktz,yt->cpqkyz", weight_first, second_factor, precision=precise)
    mode_weight = mode_weight.reshape(2, rank_local, rank_out, rows_first, -1)
    projected = jnp.einsum("cbikm,ir->cbrkm", spectrum, input_factor, precision=precise)
    rank_spectrum = lax.all_to_all(projected, "col", split_axis=2, concat_axis=1, tiled=True)
    real_part = jnp.einsum(
        "brkm,rqkm->bqkm", rank_spectrum[0], mode_weight[0], precision=precise
    ) - jnp.einsum("brkm,rqkm->bqkm", rank_spectrum[1], mode_weight[1], precision=precise)
    imag_part = jnp.einsum(
        "brkm,rqkm->bqkm", rank_spectrum[0], mode_weight[1], precision=precise
    ) + jnp.einsum("brkm,rqkm->bqkm", rank_spectrum[1], mode_weight[0], precision=precise)
    mode_values = jnp.stack([real_part, imag_part])
    summed_values = lax.psum_scatter(mode_values, "col", scatter_dimension=1, tiled=True)
    mixed_modes = jnp.einsum("oq,cbqkm->cbokm", output_factor, summed_values, precision=precise)
    return mixed_modes


def solution(mesh):
    placed = (
        P(None, "col", None, "mx", "my"),
        P(None, "col", None, ("mx", "my"), None, None),
        P(),
        P(),
        P("mx", None),
        P("my", None),
        P(),
    )
    return jax.shard_map(
        per_device,
        mesh=mesh,
        in_specs=placed,
        out_specs=P(None, "col", None, "mx", "my"),
        check_vma=False,
    )
```

profile of v0, /device:TPU:1, one launch (start us, length us, event | category | flops | bytes accessed | tf_op | source)
XLA Modules:
  0.0 377.2 jit_solution(9555578541024835973)
XLA Ops:
  6.5 0.0 copy-start
  6.5 0.0 copy-start.4
  6.5 0.0 all-gather.2.cloned.1.call-start
  6.5 1.6 copy-done
  8.1 3.9 %fusion.22 = f32[2,8,64,16,16]{2,4,3,1,0:T(8,128)} fusion(f32[2,8,64,1,16,16]{2,5,4,3,1,0:T(8,128)S(1)} %copy-done, f32[16,16]{1,0:T(8,128)} %param.13), kind=kOutput, calls=%fused_computation.17 | convolution fusion | flops 50331648 | bytes 2098176 | tf_op jit(solution)/shard_map/cpqstu,zu->cpqstz/dot_general | solution.py:17
  12.1 3.2 copy.51
  15.2 0.0 all-gather.2.cloned.1.call-update
  15.2 0.0 reduce-scatter.2.cloned.1.call-start
  15.3 0.0 copy-done.4
  15.3 3.1 fusion.26
  18.4 0.6 copy.57
  19.0 20.6 %all_to_all.15 = f32[2,2,64,8,128]{4,3,1,0,2:T(8,128)S(1)} all-to-all(f32[2,2,64,8,128]{4,3,1,0,2:T(8,128)S(1)} %copy.57), channel_id=1, replica_groups=mesh['mx'=4,'my'=4,'col'=8] {'col'}, dimensions={2} | all-to-all | bytes 2097152 | tf_op jit(solution)/shard_map/all_to_all | solution.py:29
  39.6 0.1 copy.58
  39.7 0.1 fusion.36
  39.9 0.0 copy-start.6
  39.9 3.2 copy.61
  43.1 3.1 copy.65
  46.2 90.1 %all-gather.2.cloned.1.call-done = f32[2,8,64,16,256]{4,2,1,0,3:T(8,128)} async-done(((f32[2,8,64,1,256]{4,2,1,0,3:T(8,128)}), f32[2,8,64,16,256]{4,2,1,0,3:T(8,128)}) %all-gather.2.cloned.1.call-update) | async-done | bytes 16777232 | tf_op jit(solution)/shard_map/all_gather | solution.py:21
  136.3 0.0 copy-done.6
  136.3 25.8 %fusion.16 = f32[2,8,64,8,256]{4,3,2,1,0:T(8,128)} fusion(f32[2,8,64,16,256]{4,2,1,0,3:T(8,128)} %all-gather.2.cloned.1.call-done, f32[8,16]{1,0:T(8,128)S(1)} %copy-done.6), kind=kOutput, calls=%fused_computation.15 | convolution fusion | flops 402653184 | bytes 25166336 | tf_op jit(solution)/shard_map/cpqsm,ks->cpqkm/dot_general | solution.py:22
  162.1 0.0 copy-start.7
  162.1 12.2 %copy.53 = f32[2,8,64,8,256]{2,4,3,1,0:T(8,128)} copy(f32[2,8,64,8,256]{4,3,2,1,0:T(8,128)} %fusion.16) | data formatting | bytes 16777216 | tf_op jit(solution)/shard_map/cpqsm,ks->cpqkm/transpose | solution.py:22
  174.3 0.0 copy-done.7
  174.4 17.9 %fusion.19 = f32[2,8,64,8,8,16]{2,4,5,3,1,0:T(8,128)S(1)} fusion(f32[2,8,64,8,16,16]{2,5,4,3,1,0:T(8,128)} %bitcast.59, f32[8,16]{1,0:T(8,128)S(1)} %copy-done.7), kind=kOutput, calls=%fused_computation.16 | convolution fusion | flops 201326592 | bytes 12583424 | tf_op jit(solution)/shard_map/cpqktz,yt->cpqkyz/dot_general | solution.py:26
  192.2 1.1 fusion.35
  193.3 0.9 copy.55
  194.2 0.0 copy-start.2
  194.2 0.9 copy.62
  195.2 1.2 copy-done.2
  196.4 0.0 copy-start.3
  196.4 14.4 %fusion.4 = f32[8,128,64,16]{2,3,1,0:T(8,128)S(1)} fusion(f32[16,8,8,128]{0,1,3,2:T(8,128)S(1)} %copy-done.2, f32[8,64,8,128]{1,3,2,0:T(8,128)S(1)} %bitcast.60), kind=kOutput, calls=%fused_computation.7 | convolution fusion | flops 100663296 | bytes 6815744 | tf_op jit(solution)/shard_map/brkm,rqkm->bqkm/dot_general | solution.py:33
  210.8 0.0 copy-done.3
  210.8 14.6 %fusion.6 = f32[8,128,64,16]{2,3,1,0:T(8,128)S(1)} fusion(f32[16,8,8,128]{0,1,3,2:T(8,128)S(1)} %copy-done.3, f32[8,64,8,128]{1,3,2,0:T(8,128)S(1)} %bitcast.61), kind=kOutput, calls=%fused_computation.9 | convolution fusion | flops 100663296 | bytes 6815744 | tf_op jit(solution)/shard_map/brkm,rqkm->bqkm/dot_general | solution.py:32
  225.4 14.3 %add_bitcast_fusion = f32[1,16,64,8,128]{2,1,4,3,0:T(8,128)S(1)} fusion(f32[8,128,64,16]{2,3,1,0:T(8,128)S(1)} %fusion.4, f32[16,8,8,128]{0,1,3,2:T(8,128)S(1)} %copy-done.3, f32[8,64,8,128]{1,3,2,0:T(8,128)S(1)} %bitcast.57), kind=kOutput, calls=%fused_computation.5 | convolution fusion | flops 101711872 | bytes 11010048 | tf_op jit(solution)/shard_map/brkm,rqkm->bqkm/dot_general | solution.py:35
  239.8 14.4 %subtract_bitcast_fusion = f32[1,16,64,8,128]{2,1,4,3,0:T(8,128)S(1)} fusion(f32[8,128,64,16]{2,3,1,0:T(8,128)S(1)} %fusion.6, f32[16,8,8,128]{0,1,3,2:T(8,128)S(1)} %copy-done.2, f32[8,64,8,128]{1,3,2,0:T(8,128)S(1)} %bitcast.58), kind=kOutput, calls=%fused_computation.6 | convolution fusion | flops 101711872 | bytes 11010048 | tf_op jit(solution)/shard_map/brkm,rqkm->bqkm/dot_general | solution.py:30
  254.2 6.1 %pad_maximum_fusion = f32[2,16,64,8,128]{2,1,4,3,0:T(8,128)} fusion(f32[1,16,64,8,128]{2,1,4,3,0:T(8,128)S(1)} %add_bitcast_fusion, f32[1,16,64,8,128]{2,1,4,3,0:T(8,128)S(1)} %subtract_bitcast_fusion), kind=kLoop, calls=%fused_computation | loop fusion | flops 2097152 | bytes 16777216 | tf_op jit(solution)/shard_map/stack | solution.py:36
  260.3 11.0 %copy.70 = f32[2,16,64,8,128]{4,3,2,0,1:T(8,128)} copy(f32[2,16,64,8,128]{2,1,4,3,0:T(8,128)} %pad_maximum_fusion) | data formatting | bytes 16777216 | tf_op jit(solution)/shard_map/stack | solution.py:36
  271.3 0.0 copy-start.5
  271.3 0.0 reduce-scatter.2.cloned.1.call-update
  271.3 0.0 copy-start.1
  271.3 89.9 %reduce-scatter.2.cloned.1.call-done = f32[2,2,64,8,128]{4,3,2,0,1:T(8,128)} async-done(((f32[2,16,64,8,128]{4,3,2,0,1:T(8,128)}), f32[2,2,64,8,128]{4,3,2,0,1:T(8,128)}) %reduce-scatter.2.cloned.1.call-update) | async-done | bytes 1048592 | tf_op jit(solution)/shard_map/reduce_scatter | solution.py:37
  361.2 0.0 copy-done.5
  361.2 6.0 %convolution_bitcast_fusion = f32[2,2,128,8,128]{2,4,3,1,0:T(8,128)} fusion(f32[2,2,64,8,128]{4,3,2,0,1:T(8,128)} %reduce-scatter.2.cloned.1.call-done, f32[128,64]{0,1:T(8,128)S(1)} %copy-done.5), kind=kOutput, calls=%fused_computation.21 | convolution fusion | flops 402653184 | bytes 3178496 | tf_op jit(solution)/shard_map/oq,cbqkm->cbokm/dot_general | solution.py:38
  367.2 2.9 copy.72
  370.1 0.0 copy-done.1
  (2 shorter events, 0.1 us)
Async XLA Ops:
  6.5 1.6 copy-start
  6.5 8.8 %copy-start.4 = (f32[128,64]{0,1:T(8,128)S(1)}, f32[128,64]{0,1:T(8,128)}, u32[]{:S(2)}) copy-start(f32[128,64]{0,1:T(8,128)} %param.9) | copy-start | bytes 98308
  6.5 129.7 %all-gather.2.cloned.1.call-start = ((), (), s32[]{:S(2)}) async-start(), calls=%async_computation.2 | async-start | bytes 17825792 | tf_op jit(solution)/shard_map/all_gather | solution.py:21
  15.2 346.0 %reduce-scatter.2.cloned.1.call-start = ((), (), s32[]{:S(2)}) async-start(), calls=%async_computation.3 | async-start | bytes 9437184 | tf_op jit(solution)/shard_map/reduce_scatter | solution.py:37
  39.9 96.3 %copy-start.6 = (f32[8,16]{1,0:T(8,128)S(1)}, f32[8,16]{1,0:T(8,128)}, u32[]{:S(2)}) copy-start(f32[8,16]{1,0:T(8,128)} %param.11) | copy-start | bytes 1540
  162.1 12.2 %copy-start.7 = (f32[8,16]{1,0:T(8,128)S(1)}, f32[8,16]{1,0:T(8,128)}, u32[]{:S(2)}) copy-start(f32[8,16]{1,0:T(8,128)} %param.12) | copy-start | bytes 1540
  194.2 2.2 copy-start.2
  196.4 14.4 %copy-start.3 = (f32[16,8,8,128]{0,1,3,2:T(8,128)S(1)}, f32[16,8,8,128]{0,1,3,2:T(8,128)}, u32[]{:S(2)}) copy-start(f32[16,8,8,128]{0,1,3,2:T(8,128)} %copy.65) | copy-start | bytes 1572868
  271.3 89.9 %copy-start.5 = (f32[128,64]{0,1:T(8,128)S(1)}, f32[128,64]{0,1:T(8,128)}, u32[]{:S(2)}) copy-start(f32[128,64]{0,1:T(8,128)} %param.10) | copy-start | bytes 98308
  271.3 98.8 %copy-start.1 = (f32[2,8,64,1,16,16]{2,5,4,3,1,0:T(8,128)S(1)}, f32[2,8,64,1,16,16]{2,5,4,3,1,0:T(8,128)}, u32[]{:S(2)}) copy-start(f32[2,8,64,1,16,16]{2,5,4,3,1,0:T(8,128)} %param.8) | copy-start | bytes 3145732
Sparse Core Ops, SparseCore 0:
  15.4 120.8 all-gather.1
  271.4 89.7 reduce-scatter.1
where the time goes:
time: 383 us; the launch traced here: 377 us
  waiting for transfers between devices  180 us (47%)
  matrix products  114 us (30%)
  local copies, waits for them, and re-layouts  42.2 us (11%)
  blocking collectives  20.6 us (5%)
  between operations  13.8 us (4%)
  other arithmetic  6.1 us (2%)
    all_gather x1, waiting for transfers between devices, per_device(): core_gathered = lax.all_gather(core_third, ('mx', 'my'), axis=3, tiled=True)  90.1 us
    reduce_scatter x1, waiting for transfers between devices, per_device(): lax.psum_scatter(mode_values, 'col', scatter_dimension=1, tiled=True)  89.9 us
    dot_general x1, matrix products, per_device(): jnp.einsum('cpqsm,ks->cpqkm', core_gathered, first_factor, precision=prec...  25.8 us
    all_to_all x1, blocking collectives, per_device(): lax.all_to_all(projected, 'col', split_axis=2, concat_axis=1, tiled=True)  20.6 us
    dot_general x1, matrix products, per_device(): jnp.einsum('cpqktz,yt->cpqkyz', weight_first, second_factor, precision=pr...  17.9 us
    dot_general x1, matrix products, per_device(): jnp.einsum('brkm,rqkm->bqkm', rank_spectrum[1], mode_weight[1], precision...  14.6 us
    dot_general x1, matrix products, per_device(): jnp.einsum('brkm,rqkm->bqkm', rank_spectrum[0], mode_weight[1], precision...  14.4 us
    dot_general x1, matrix products, per_device(): jnp.einsum('brkm,rqkm->bqkm', rank_spectrum[0], mode_weight[0], precision...  14.4 us
  transfers between devices with their start and end apart: 2, of which 2 were waited for; matrix products, arithmetic and copies ran while one was open for 3% of the time, Pallas kernels for 0%

commit v1 on v0

--- a/solution.py
+++ b/solution.py
@@ -18,7 +18,10 @@
     core_third = core_third.reshape(
         2, rank_local, rank_out, core_tensor.shape[3], rank_second * modes_third
     )
-    core_gathered = lax.all_gather(core_third, ("mx", "my"), axis=3, tiled=True)
+    core_gathered = jnp.concatenate(
+        lax.all_to_all(jnp.stack([core_third] * lax.axis_size(("mx", "my"))), ("mx", "my"), 0, 0),
+        axis=3,
+    )
     weight_first = jnp.einsum("cpqsm,ks->cpqkm", core_gathered, first_factor, precision=precise)
     weight_first = weight_first.reshape(
         2, rank_local, rank_out, rows_first, rank_second, modes_third

time: 383 us -> 485 us (1.27)
  waiting for transfers between devices: 180 us -> 278 us
  blocking collectives: 20.6 us -> 0 us
  starting transfers between devices: 0.04 us -> 14.3 us
  local copies, waits for them, and re-layouts: 42.2 us -> 49.9 us
    all_to_all x0 -> x2, waiting for transfers between devices: none -> 190 us  [the longest x1 178 us: per_device(): lax.all_to_all(jnp.stack([core_third] * lax.axis_size(('mx', 'my'))), ('m...]
    all_gather x1 -> x0, waiting for transfers between devices: 90.1 us -> none  [per_device(): core_gathered = lax.all_gather(core_third, ('mx', 'my'), axis=3, tiled=True)]
    all_to_all x1 -> x0, blocking collectives: 20.6 us -> none  [per_device(): lax.all_to_all(projected, 'col', split_axis=2, concat_axis=1, tiled=True)]
    all_to_all x0 -> x2, starting transfers between devices: none -> 14.3 us  [the longest x1 8.45 us: per_device(): lax.all_to_all(jnp.stack([core_third] * lax.axis_size(('mx', 'my'))), ('m...]
    another operation x0 -> x2, local copies, waits for them, and re-layouts: none -> 8.44 us  [per_device(): jnp.stack([core_third] * lax.axis_size(('mx', 'my')))]
  transfers between devices with their start and end apart: 2 -> 3, of which waited for: 2 -> 3; matrix products, arithmetic and copies ran while one was open for 3% -> 3% of each run, Pallas kernels for 0% -> 0%
where the time goes in v1:
time: 485 us; the launch traced here: 478 us
  waiting for transfers between devices  278 us (57%)
  matrix products  115 us (24%)
  local copies, waits for them, and re-layouts  49.9 us (10%)
  starting transfers between devices  14.3 us (3%)
  between operations  14.1 us (3%)
  other arithmetic  6.12 us (1%)
    all_to_all x1, waiting for transfers between devices, per_device(): lax.all_to_all(jnp.stack([core_third] * lax.axis_size(('mx', 'my'))), ('m...  178 us
    reduce_scatter x1, waiting for transfers between devices, per_device(): lax.psum_scatter(mode_values, 'col', scatter_dimension=1, tiled=True)  88.4 us
    dot_general x1, matrix products, per_device(): jnp.einsum('cpqsm,ks->cpqkm', core_gathered, first_factor, precision=prec...  25.9 us
    dot_general x1, matrix products, per_device(): jnp.einsum('cpqktz,yt->cpqkyz', weight_first, second_factor, precision=pr...  17.9 us
    dot_general x1, matrix products, per_device(): jnp.einsum('brkm,rqkm->bqkm', rank_spectrum[0], mode_weight[0], precision...  16.3 us
    dot_general x1, matrix products, per_device(): jnp.einsum('brkm,rqkm->bqkm', rank_spectrum[1], mode_weight[1], precision...  14.6 us
    dot_general x1, matrix products, per_device(): jnp.einsum('brkm,rqkm->bqkm', rank_spectrum[1], mode_weight[0], precision...  14.4 us
    dot_general x1, matrix products, per_device(): jnp.einsum('brkm,rqkm->bqkm', rank_spectrum[0], mode_weight[1], precision...  14.3 us
  transfers between devices with their start and end apart: 3, of which 3 were waited for; matrix products, arithmetic and copies ran while one was open for 3% of the time, Pallas kernels for 0%

profile of v1, /device:TPU:1, one launch (start us, length us, event | category | flops | bytes accessed | tf_op | source)
XLA Modules:
  0.0 477.7 jit_solution(11799865904743419519)
XLA Ops:
  6.5 0.0 copy-start
  6.5 0.0 copy-start.6
  6.5 1.6 copy-done
  8.1 2.3 fusion.27
  10.4 1.6 copy.57
  12.0 5.9 %all-to-all-start.1 = ((f32[2,2,64,8,128]{4,3,1,0,2:T(8,128)}), f32[2,2,64,8,128]{4,3,1,0,2:T(8,128)}, u32[]{:S(2)}, u32[]{:S(2)}) async-start(f32[2,2,64,8,128]{4,3,1,0,2:T(8,128)} %copy.57), calls=%async_computation.1 | async-start | bytes 2097152 | tf_op jit(solution)/shard_map/all_to_all | solution.py:32
  17.9 0.0 copy-done.6
  17.9 3.5 fusion.23
  21.4 0.6 copy.51
  22.0 11.9 %all-to-all-done.1 = f32[2,2,64,8,128]{4,3,1,0,2:T(8,128)} async-done(((f32[2,2,64,8,128]{4,3,1,0,2:T(8,128)}), f32[2,2,64,8,128]{4,3,1,0,2:T(8,128)}, u32[]{:S(2)}, u32[]{:S(2)}) %all-to-all-start.1) | async-done | bytes 1048608 | tf_op jit(solution)/shard_map/all_to_all | solution.py:32
  33.8 7.9 %stack.12 = f32[16,2,8,64,1,256]{5,3,2,1,4,0:T(8,128)} broadcast(f32[2,8,64,256]{3,2,1,0:T(8,128)S(1)} %copy.51), dimensions={1,2,3,5} | broadcast | bytes 17825792 | tf_op jit(solution)/shard_map/stack | solution.py:22
  41.7 8.5 %all-to-all-start = ((f32[16,2,8,64,1,256]{5,3,2,1,4,0:T(8,128)}), f32[16,2,8,64,1,256]{5,3,2,1,4,0:T(8,128)}, u32[]{:S(2)}, u32[]{:S(2)}) async-start(f32[16,2,8,64,1,256]{5,3,2,1,4,0:T(8,128)} %stack.12), calls=%async_computation | async-start | bytes 33554432 | tf_op jit(solution)/shard_map/all_to_all | solution.py:22
  50.1 0.0 reduce-scatter.2.cloned.1.call-start
  50.2 1.3 copy.58
  51.5 0.1 fusion.37
  51.6 0.0 copy-start.7
  51.6 3.1 copy.65
  54.8 3.2 copy.61
  58.1 177.8 %all-to-all-done = f32[16,2,8,64,1,256]{5,3,2,1,4,0:T(8,128)} async-done(((f32[16,2,8,64,1,256]{5,3,2,1,4,0:T(8,128)}), f32[16,2,8,64,1,256]{5,3,2,1,4,0:T(8,128)}, u32[]{:S(2)}, u32[]{:S(2)}) %all-to-all-start) | async-done | bytes 16777248 | tf_op jit(solution)/shard_map/all_to_all | solution.py:22
  235.9 0.0 copy-done.7
  235.9 25.9 %fusion.20 = f32[2,8,64,8,256]{4,3,2,1,0:T(8,128)} fusion(f32[16,2,8,64,1,256]{5,3,2,1,4,0:T(8,128)} %all-to-all-done, f32[8,16]{1,0:T(8,128)S(1)} %copy-done.7), kind=kOutput, calls=%fused_computation.17 | convolution fusion | flops 402653184 | bytes 25166336 | tf_op jit(solution)/shard_map/cpqsm,ks->cpqkm/dot_general | solution.py:25
  261.8 0.0 copy-start.8
  261.8 12.2 %copy.53 = f32[2,8,64,8,256]{2,4,3,1,0:T(8,128)} copy(f32[2,8,64,8,256]{4,3,2,1,0:T(8,128)} %fusion.20) | data formatting | bytes 16777216 | tf_op jit(solution)/shard_map/cpqsm,ks->cpqkm/transpose | solution.py:25
  274.0 0.0 copy-done.8
  274.0 17.9 %fusion.17 = f32[2,8,64,8,8,16]{2,4,5,3,1,0:T(8,128)S(1)} fusion(f32[2,8,64,8,16,16]{2,5,4,3,1,0:T(8,128)} %bitcast.66, f32[8,16]{1,0:T(8,128)S(1)} %copy-done.8), kind=kOutput, calls=%fused_computation.16 | convolution fusion | flops 201326592 | bytes 12583424 | tf_op jit(solution)/shard_map/cpqktz,yt->cpqkyz/dot_general | solution.py:29
  291.9 1.1 fusion.36
  293.0 0.9 copy.62
  294.0 0.0 copy-start.2
  294.0 0.9 copy.55
  294.9 1.2 copy-done.2
  296.2 0.0 copy-start.3
  296.2 14.6 %fusion.7 = f32[8,128,64,16]{2,3,1,0:T(8,128)S(1)} fusion(f32[16,8,8,128]{0,1,3,2:T(8,128)S(1)} %copy-done.2, f32[8,64,8,128]{1,3,2,0:T(8,128)S(1)} %bitcast.67), kind=kOutput, calls=%fused_computation.10 | convolution fusion | flops 100663296 | bytes 6815744 | tf_op jit(solution)/shard_map/brkm,rqkm->bqkm/dot_general | solution.py:35
  310.8 0.0 copy-done.3
  310.8 14.3 %fusion.5 = f32[8,128,64,16]{2,3,1,0:T(8,128)S(1)} fusion(f32[16,8,8,128]{0,1,3,2:T(8,128)S(1)} %copy-done.3, f32[8,64,8,128]{1,3,2,0:T(8,128)S(1)} %bitcast.68), kind=kOutput, calls=%fused_computation.8 | convolution fusion | flops 100663296 | bytes 6815744 | tf_op jit(solution)/shard_map/brkm,rqkm->bqkm/dot_general | solution.py:36
  325.1 16.3 %subtract_bitcast_fusion = f32[1,16,64,8,128]{2,1,4,3,0:T(8,128)} fusion(f32[8,128,64,16]{2,3,1,0:T(8,128)S(1)} %fusion.7, f32[16,8,8,128]{0,1,3,2:T(8,128)S(1)} %copy-done.3, f32[8,64,8,128]{1,3,2,0:T(8,128)S(1)} %bitcast.64), kind=kOutput, calls=%fused_computation.7 | convolution fusion | flops 101711872 | bytes 11010048 | tf_op jit(solution)/shard_map/brkm,rqkm->bqkm/dot_general | solution.py:33
  341.4 0.0 copy-start.4
  341.4 14.4 %add_bitcast_fusion = f32[1,16,64,8,128]{2,1,4,3,0:T(8,128)S(1)} fusion(f32[8,128,64,16]{2,3,1,0:T(8,128)S(1)} %fusion.5, f32[16,8,8,128]{0,1,3,2:T(8,128)S(1)} %copy-done.2, f32[8,64,8,128]{1,3,2,0:T(8,128)S(1)} %bitcast.65), kind=kOutput, calls=%fused_computation.6 | convolution fusion | flops 101711872 | bytes 11010048 | tf_op jit(solution)/shard_map/brkm,rqkm->bqkm/dot_general | solution.py:38
  355.8 0.0 copy-done.4
  355.8 6.1 %pad_maximum_fusion = f32[2,16,64,8,128]{2,1,4,3,0:T(8,128)} fusion(f32[1,16,64,8,128]{2,1,4,3,0:T(8,128)S(1)} %add_bitcast_fusion, f32[1,16,64,8,128]{2,1,4,3,0:T(8,128)S(1)} %copy-done.4), kind=kLoop, calls=%fused_computation | loop fusion | flops 2097152 | bytes 16777216 | tf_op jit(solution)/shard_map/stack | solution.py:39
  362.0 11.1 %copy.70 = f32[2,16,64,8,128]{4,3,2,0,1:T(8,128)} copy(f32[2,16,64,8,128]{2,1,4,3,0:T(8,128)} %pad_maximum_fusion) | data formatting | bytes 16777216 | tf_op jit(solution)/shard_map/stack | solution.py:39
  373.0 0.0 copy-start.5
  373.0 0.0 reduce-scatter.2.cloned.1.call-update
  373.1 0.0 copy-start.1
  373.1 88.4 %reduce-scatter.2.cloned.1.call-done = f32[2,2,64,8,128]{4,3,2,0,1:T(8,128)} async-done(((f32[2,16,64,8,128]{4,3,2,0,1:T(8,128)}), f32[2,2,64,8,128]{4,3,2,0,1:T(8,128)}) %reduce-scatter.2.cloned.1.call-update) | async-done | bytes 1048592 | tf_op jit(solution)/shard_map/reduce_scatter | solution.py:40
  461.5 0.0 copy-done.5
  461.5 6.0 %convolution_bitcast_fusion = f32[2,2,128,8,128]{2,4,3,1,0:T(8,128)} fusion(f32[2,2,64,8,128]{4,3,2,0,1:T(8,128)} %reduce-scatter.2.cloned.1.call-done, f32[128,64]{0,1:T(8,128)S(1)} %copy-done.5), kind=kOutput, calls=%fused_computation.22 | convolution fusion | flops 402653184 | bytes 3178496 | tf_op jit(solution)/shard_map/oq,cbqkm->cbokm/dot_general | solution.py:41
  467.5 2.9 copy.72
  470.4 0.0 copy-done.1
  (2 shorter events, 0.1 us)
Async XLA Ops:
  6.5 1.6 copy-start
  6.5 11.3 %copy-start.6 = (f32[16,16]{1,0:T(8,128)S(1)}, f32[16,16]{1,0:T(8,128)}, u32[]{:S(2)}) copy-start(f32[16,16]{1,0:T(8,128)} %param.13) | copy-start | bytes 3076
  12.0 21.8 %all-to-all-start.1 = ((f32[2,2,64,8,128]{4,3,1,0,2:T(8,128)}), f32[2,2,64,8,128]{4,3,1,0,2:T(8,128)}, u32[]{:S(2)}, u32[]{:S(2)}) async-start(f32[2,2,64,8,128]{4,3,1,0,2:T(8,128)} %copy.57), calls=%async_computation.1 | async-start | bytes 2097152 | tf_op jit(solution)/shard_map/all_to_all | solution.py:32
  41.7 194.2 %all-to-all-start = ((f32[16,2,8,64,1,256]{5,3,2,1,4,0:T(8,128)}), f32[16,2,8,64,1,256]{5,3,2,1,4,0:T(8,128)}, u32[]{:S(2)}, u32[]{:S(2)}) async-start(f32[16,2,8,64,1,256]{5,3,2,1,4,0:T(8,128)} %stack.12), calls=%async_computation | async-start | bytes 33554432 | tf_op jit(solution)/shard_map/all_to_all | solution.py:22
  50.1 411.3 %reduce-scatter.2.cloned.1.call-start = ((), (), s32[]{:S(2)}) async-start(), calls=%async_computation.3 | async-start | bytes 9437184 | tf_op jit(solution)/shard_map/reduce_scatter | solution.py:40
  51.6 184.2 %copy-start.7 = (f32[8,16]{1,0:T(8,128)S(1)}, f32[8,16]{1,0:T(8,128)}, u32[]{:S(2)}) copy-start(f32[8,16]{1,0:T(8,128)} %param.11) | copy-start | bytes 1540
  261.8 12.2 %copy-start.8 = (f32[8,16]{1,0:T(8,128)S(1)}, f32[8,16]{1,0:T(8,128)}, u32[]{:S(2)}) copy-start(f32[8,16]{1,0:T(8,128)} %param.12) | copy-start | bytes 1540
  294.0 2.2 copy-start.2
  296.2 14.6 %copy-start.3 = (f32[16,8,8,128]{0,1,3,2:T(8,128)S(1)}, f32[16,8,8,128]{0,1,3,2:T(8,128)}, u32[]{:S(2)}) copy-start(f32[16,8,8,128]{0,1,3,2:T(8,128)} %copy.61) | copy-start | bytes 1572868
  341.4 14.4 %copy-start.4 = (f32[1,16,64,8,128]{2,1,4,3,0:T(8,128)S(1)}, f32[1,16,64,8,128]{2,1,4,3,0:T(8,128)}, u32[]{:S(2)}) copy-start(f32[1,16,64,8,128]{2,1,4,3,0:T(8,128)} %subtract_bitcast_fusion) | copy-start | bytes 12582916
  373.0 88.5 %copy-start.5 = (f32[128,64]{0,1:T(8,128)S(1)}, f32[128,64]{0,1:T(8,128)}, u32[]{:S(2)}) copy-start(f32[128,64]{0,1:T(8,128)} %param.10) | copy-start | bytes 98308
  373.1 97.3 %copy-start.1 = (f32[2,2,128,8,128]{4,3,2,1,0:T(8,128)S(1)}, f32[2,2,128,8,128]{4,3,2,1,0:T(8,128)}, u32[]{:S(2)}) copy-start(f32[2,2,128,8,128]{4,3,2,1,0:T(8,128)} %param.7) | copy-start | bytes 6291460
Sparse Core Ops, SparseCore 0:
  373.2 88.2 reduce-scatter.1
